TPU v7x, 256 devices: a whole 4x4x8 slice. The times are simulated.
256 devices in a mesh: blk: 16 (over x_lo, z), tgt: 16 (over y, x_hi, core).
Axes of the slice: x: 4 (x_hi: 2, x_lo: 2; x = x_hi * 2 + x_lo), y: 4, z: 8, core: 2. Of those that a mesh axis runs over, the one named last changes fastest.
Arguments:
- sources: float32 [16384, 128], P('blk'), may hold values from -0.5 to 0.5, as said below
- targets: float32 [65536, 128], P(('blk', 'tgt')), may hold values from -0.5 to 0.5, as said below
- duals_init: float32 [65536], P(('blk', 'tgt')), may hold values from -1.5 to 1.5
Outputs:
- source_duals: float32 [16384], P('blk')
- target_duals: float32 [65536], P(('blk', 'tgt'))
Inputs may be any that keep to these rules, and one draw needn't show every extreme that they name: `sources`: coordinates of the source points. `targets`: coordinates of the target points.
All inputs are finite; a program needn't handle non-finite values.
Results may differ from a plain program's by a relative error of at most 0.0001.
Values sent between devices are 32-bit elements; how exact they have to be, the bound alone decides.
No kernel may reach another device: no remote copies, remote signals or barrier semaphores. Data moves between devices by JAX's collectives and lax.ppermute only.
A program may use at most 64 MiB of HBM per device.

v0:
```python
import functools
import math

import jax
import jax.numpy as jnp
from jax import lax
from jax.experimental import pallas as pl
from jax.experimental.pallas import tpu as pltpu
from jax.sharding import Mesh
from jax.sharding import PartitionSpec as P


EPS = 0.05
SCALE = math.log2(math.e) / EPS
LOG2E = math.log2(math.e)
N_SRC = 16384
N_DST = 65536
ROWS = 1024
COLS = 256
RING = 8
PLANE = 32
LANES = 128
TILES = ROWS // LANES
MIB = 1024 * 1024

BLK = ("xl", "z")
TGT = ("y", "xh", "core")
PLANE_AXES = ("xl", "y", "xh", "core")

VMEM = pl.BlockSpec(memory_space=pltpu.VMEM)


def log2(x):
    return jnp.log(x) * LOG2E


def diagonal():
    shape = (LANES, LANES)
    return lax.broadcasted_iota(jnp.int32, shape, 0) == lax.broadcasted_iota(jnp.int32, shape, 1)


def as_column(eye, row):
    return jnp.sum(jnp.where(eye, row, 0.0), axis=1, keepdims=True)


def as_row(eye, column):
    return jnp.sum(jnp.where(eye, column, 0.0), axis=0, keepdims=True)


def tree(op, parts):
    parts = list(parts)
    while len(parts) > 1:
        parts = [op(*parts[k : k + 2]) if k + 1 < len(parts) else parts[k] for k in range(0, len(parts), 2)]
    return parts[0]


def three_parts(x):
    high = x.astype(jnp.bfloat16)
    rest = x - high.astype(jnp.float32)
    mid = rest.astype(jnp.bfloat16)
    low = (rest - mid.astype(jnp.float32)).astype(jnp.bfloat16)
    return high, mid, low


def online(scores, state):
    high = tree(jnp.maximum, scores)
    if state is None:
        return high, tree(jnp.add, [jnp.exp2(s - high) for s in scores])
    high = jnp.maximum(high, state[0])
    total = tree(jnp.add, [jnp.exp2(s - high) for s in scores])
    return high, state[1] * jnp.exp2(state[0] - high) + total


def over_sublanes(high, total):
    top = jnp.max(high, axis=0, keepdims=True)
    return top + log2(jnp.sum(total * jnp.exp2(high - top), axis=0, keepdims=True))


def joined(parts):
    top = jnp.max(parts, axis=0)
    return top + log2(jnp.sum(jnp.exp2(parts - top[None]), axis=0))


def put_rows(rows_ref, state_of):
    for half in range(2):
        lse = jnp.concatenate([over_sublanes(*state_of(half, t)) for t in range(TILES)], axis=0)
        for peer in range(PLANE):
            rows_ref[peer, half] = lse


def prepare_sources(x, half, x_ref):
    turned = (x * (2.0 * SCALE)).T
    high, mid, low = three_parts(turned)
    for k, part in enumerate((high, high, mid, mid, low, high)):
        x_ref[half, k * LANES : (k + 1) * LANES, :] = part


def prepare_targets(eye, block_ref, pots_ref):
    y = block_ref[0:COLS, :]
    norms = jnp.sum(y * y, axis=1, keepdims=True)
    for c in range(COLS // LANES):
        rows = slice(c * LANES, (c + 1) * LANES)
        column = as_column(eye, block_ref[COLS + c : COLS + c + 1, :])
        pots_ref[rows, :] = jnp.broadcast_to((column - norms[rows]) * SCALE, (LANES, LANES))
    high, mid, low = three_parts(y)
    return jnp.concatenate([high, mid, high, mid, high, low], axis=1), norms


def add_block(parts, pots_ref, at, half, x_ref, tile_ref, state_ref, fresh):
    step = 512
    for n in range(ROWS // step):
        lanes = slice(n * step, (n + 1) * step)
        tile_ref[at, half, :, lanes] = jnp.dot(parts, x_ref[half, :, lanes], preferred_element_type=jnp.float32)
        for t in range(n * step // LANES, (n + 1) * step // LANES):
            tile = slice(t * LANES, (t + 1) * LANES)
            state = None if fresh else (state_ref[0, half, :, tile], state_ref[1, half, :, tile])
            for c in range(0, COLS, 64):
                rows = range(c, c + 64, 8)
                state = online([tile_ref[at, half, r : r + 8, tile] + pots_ref[r : r + 8, :] for r in rows], state)
            state_ref[0, half, :, tile], state_ref[1, half, :, tile] = state


def ring_index(z, offset):
    return lax.rem(z + jnp.where(lax.rem(z, 2) == 0, offset, -offset) + RING, RING)


def start_kernel(sources_ref, block_ref, tile_ref, x_ref, state_ref, src_norm_ref, dst_norm_ref, pots_scr):
    z, mine = lax.axis_index("z"), lax.axis_index("xl")
    eye = diagonal()
    x = sources_ref[...]
    prepare_sources(x, mine, x_ref)
    squares = jnp.sum(x * x, axis=1, keepdims=True)
    for c in range(TILES):
        src_norm_ref[c : c + 1, :] = as_row(eye, squares[c * LANES : (c + 1) * LANES])
    parts, norms = prepare_targets(eye, block_ref, pots_scr)
    for c in range(COLS // LANES):
        dst_norm_ref[c : c + 1, :] = as_row(eye, norms[c * LANES : (c + 1) * LANES])
    add_block(parts, pots_scr, z, mine, x_ref, tile_ref, state_ref, True)


def own_kernel(offsets, x_ref, *refs):
    blocks, (tile_ref, state_ref), pots_scr = refs[: len(offsets)], refs[-3:-1], refs[-1]
    z, mine = lax.axis_index("z"), lax.axis_index("xl")
    eye = diagonal()
    for b, offset in enumerate(offsets):
        parts, _ = prepare_targets(eye, blocks[b], pots_scr.at[b])
        add_block(parts, pots_scr.at[b], ring_index(z, offset), mine, x_ref, tile_ref, state_ref, False)


def partner_kernel(fresh, work, *refs):
    refs = list(refs)
    sources_ref = refs.pop(0) if fresh else None
    blocks, (tile_ref, x_ref, state_ref), pots_scr = refs[: len(work)], refs[-4:-1], refs[-1]
    z, mine = lax.axis_index("z"), lax.axis_index("xl")
    eye = diagonal()
    if fresh:
        prepare_sources(sources_ref[...], 1 - mine, x_ref)
    for b, (offset, own, partner) in enumerate(work):
        parts, _ = prepare_targets(eye, blocks[b], pots_scr.at[b])
        at = ring_index(z, offset)
        if own:
            add_block(parts, pots_scr.at[b], at, mine, x_ref, tile_ref, state_ref, False)
        if partner:
            add_block(parts, pots_scr.at[b], at, 1 - mine, x_ref, tile_ref, state_ref, fresh and b == 0)


def last_kernel(offset, x_ref, block_ref, *refs):
    (tile_ref, state_ref, rows_ref), pots_scr = refs[-4:-1], refs[-1]
    parts, _ = prepare_targets(diagonal(), block_ref, pots_scr)
    for half in range(2):
        add_block(parts, pots_scr, ring_index(lax.axis_index("z"), offset), half, x_ref, tile_ref, state_ref, False)
    tiles = [slice(t * LANES, (t + 1) * LANES) for t in range(TILES)]
    put_rows(rows_ref, lambda half, t: (state_ref[0, half, :, tiles[t]], state_ref[1, half, :, tiles[t]]))


F32 = jnp.float32
TILE = jax.ShapeDtypeStruct((RING, 2, COLS, ROWS + LANES), F32)
PARTS = jax.ShapeDtypeStruct((2, 6 * LANES, ROWS), jnp.bfloat16)
STATE = jax.ShapeDtypeStruct((2, 2, 8, ROWS), F32)
ROW_LSE = jax.ShapeDtypeStruct((PLANE, 2, TILES, LANES), F32)


def call(kernel, args, outs, blocks, scratch=(), aliases={}):
    return pl.pallas_call(
        kernel,
        out_shape=outs,
        in_specs=[VMEM] * len(args),
        out_specs=[VMEM] * len(outs),
        scratch_shapes=list(scratch),
        input_output_aliases=aliases,
        compiler_params=pltpu.CompilerParams(vmem_limit_bytes=24 * MIB),
        cost_estimate=pl.CostEstimate(
            flops=blocks * 2 * COLS * ROWS * 768, bytes_accessed=MIB, transcendentals=blocks * COLS * ROWS
        ),
    )(*args)


def pick_kernel(plus_ref, minus_ref, far_ref):
    odd = lax.rem(lax.axis_index("z") + lax.axis_index("core"), 2) == 1
    far_ref[...] = jnp.where(odd, plus_ref[...], minus_ref[...])


def from_afar(plus, minus):
    (block,) = call(pick_kernel, (plus, minus), [jax.ShapeDtypeStruct(plus.shape, F32)], 0)
    pairs = [(2 * z + c, 2 * ((z + (2, -2)[c]) % RING) + c) for z in range(RING) for c in range(2)]
    return lax.ppermute(block, ("z", "core"), pairs)


def columns_kernel(copies, rows_ref, src_norm_ref, tile_ref, *refs):
    if copies:
        cols_ref, part_scr, turned_scr = refs
    else:
        cols_ref, source_pots_ref, part_scr, turned_scr = refs
    u = -math.log2(N_DST) - joined(rows_ref[...])
    if not copies:
        mine = lax.axis_index("xl")
        own = jnp.where(mine == 0, u[0], u[1])
        source_pots_ref[...] = own * (1.0 / SCALE) + src_norm_ref[...]
    pots = [jnp.broadcast_to(u[h, t : t + 1, :], (8, LANES)) for h in range(2) for t in range(TILES)]
    groups = 32
    turns = COLS // 8 // groups

    def load(i, g, h):
        k, first = i // turns, lax.rem(i, turns) * (8 * groups)
        rows = pl.ds(pl.multiple_of(first + 8 * g, 8), 8)
        scores = [tile_ref[k, h, rows, t * LANES : (t + 1) * LANES] + pots[h * TILES + t] for t in range(TILES)]
        return tree(jnp.maximum, scores), scores

    def turn(k, quarter):
        turned_scr[k, quarter] = part_scr[k, quarter].T

    def body(i, held):
        k, place = i // turns, lax.rem(i, turns)
        for quarter in range(4 // turns):
            turn(jnp.maximum(k - 1, 0), place * (4 // turns) + quarter)
        for g in range(groups):
            following = load(i, g, 1)
            high, scores = held
            total = tree(jnp.add, [jnp.exp2(s - high) for s in scores])
            held = following
            following = load(i, g + 1, 0) if g + 1 < groups else load(jnp.minimum(i + 1, RING * turns - 1), 0, 0)
            both, scores = jnp.maximum(high, held[0]), held[1]
            total = total * jnp.exp2(high - both) + tree(jnp.add, [jnp.exp2(s - both) for s in scores])
            half, rows = place + g // 16, slice(8 * (g % 16), 8 * (g % 16) + 8)
            part_scr[k, half, rows, :] = both
            part_scr[k, 2 + half, rows, :] = total
            held = following
        return held

    lax.fori_loop(0, RING * turns, body, load(0, 0, 0))
    for quarter in range(4):
        turn(RING - 1, quarter)
    for k in range(RING):
        for c in range(2):
            high = turned_scr[k, c]
            top = jnp.max(high, axis=0, keepdims=True)
            total = jnp.sum(turned_scr[k, 2 + c] * jnp.exp2(high - top), axis=0, keepdims=True)
            lse = top + log2(total)
            if copies:
                for peer in range(RING):
                    cols_ref[peer, 2 * k + c : 2 * k + c + 1, :] = lse
            else:
                cols_ref[k, c : c + 1, :] = lse


def columns(rows, src_norm, tile, copies):
    if copies:
        outs = [jax.ShapeDtypeStruct((RING, RING * 2, LANES), F32)]
    else:
        outs = [jax.ShapeDtypeStruct((RING, 2, LANES), F32), jax.ShapeDtypeStruct((TILES, LANES), F32)]
    scratch = [pltpu.VMEM((RING, 4, LANES, LANES), F32)] * 2
    return call(functools.partial(columns_kernel, copies), (rows, src_norm, tile), outs, 16, scratch)


def rows_kernel(cols_ref, tile_ref, rows_ref, w_scr, pots_scr, high_scr, total_scr):
    eye = diagonal()
    w = -math.log2(N_SRC) - joined(cols_ref[...])
    for r in range(2 * RING):
        w_scr[r] = w[r : r + 1, :]
    high_scr[...] = jnp.full_like(high_scr, -3.0e38)
    total_scr[...] = jnp.zeros_like(total_scr)
    unit = 8
    count = COLS // 8 // unit

    def spread(k):
        for c in range(2):
            pots_scr[k, c * LANES : (c + 1) * LANES, :] = jnp.broadcast_to(as_column(eye, w_scr[2 * k + c]), (LANES, LANES))

    def load(k, tile, part):
        half, t = divmod(tile, TILES)
        lanes = slice(t * LANES, (t + 1) * LANES)
        rows = [slice(8 * r, 8 * r + 8) for r in range(part * unit, (part + 1) * unit)]
        scores = [tile_ref[k, half, r, lanes] + pots_scr[k, r, :] for r in rows]
        return tree(jnp.maximum, scores), scores

    def body(k, held):
        for tile in range(2 * TILES):
            before, total = high_scr[tile], total_scr[tile]
            for part in range(count):
                if part + 1 < count:
                    following = load(k, tile, part + 1)
                elif tile + 1 < 2 * TILES:
                    following = load(k, tile + 1, 0)
                else:
                    following = load(jnp.minimum(k + 1, RING - 1), 0, 0)
                high, scores = jnp.maximum(held[0], before), held[1]
                total = total * jnp.exp2(before - high) + tree(jnp.add, [jnp.exp2(s - high) for s in scores])
                before, held = high, following
            high_scr[tile], total_scr[tile] = before, total
        spread(jnp.minimum(k + 2, RING - 1))
        return held

    spread(0)
    spread(1)
    lax.fori_loop(0, RING, body, load(0, 0, 0))
    put_rows(rows_ref, lambda half, tile: (high_scr[half * TILES + tile], total_scr[half * TILES + tile]))


def rows(cols, tile):
    scratch = [
        pltpu.VMEM((2 * RING, 1, LANES), F32),
        pltpu.VMEM((RING, COLS, LANES), F32),
        pltpu.VMEM((2 * TILES, 8, LANES), F32),
        pltpu.VMEM((2 * TILES, 8, LANES), F32),
    ]
    return call(rows_kernel, (cols, tile), [ROW_LSE], 16, scratch)[0]


def shifted(x, axis, by):
    count = lax.axis_size(axis)
    return lax.ppermute(x, axis, [(i, (i + by) % count) for i in range(count)])


def swapped(x, first):
    pairs = [(z, (z + (1 if z % 2 == first else -1)) % RING) for z in range(RING)]
    return lax.ppermute(x, "z", pairs)


def over_plane(copies):
    return lax.all_to_all(copies, PLANE_AXES, 0, 0, tiled=True)


def steps(sources, targets, duals_init):
    packed = jnp.concatenate([targets, jnp.pad(duals_init.reshape(2, LANES), ((0, 6), (0, 0)))], axis=0)
    plus, minus = [packed], [packed]
    for _ in range(1, RING // 2):
        from_pair = swapped(minus[-1], 0)
        minus.append(swapped(plus[-1], 1))
        plus.append(from_pair)
    far = from_afar(plus[2], minus[2])
    others = shifted(sources, "xl", 1)
    pots = pltpu.VMEM((COLS, LANES), F32)
    norms = [jax.ShapeDtypeStruct((TILES, LANES), F32), jax.ShapeDtypeStruct((2, LANES), F32)]
    tile, x, state, src_norm, dst_norm = call(start_kernel, (sources, packed), [TILE, PARTS, STATE, *norms], 1, [pots])

    def own(step):
        return call(
            functools.partial(own_kernel, (-step, step)),
            (x, minus[step], plus[step], tile, state),
            [TILE, STATE],
            2,
            [pltpu.VMEM((2, COLS, LANES), F32)],
            {3: 0, 4: 1},
        )

    def partner(fresh, work, *blocks):
        first = (others,) if fresh else ()
        at = len(first) + len(blocks)
        return call(
            functools.partial(partner_kernel, fresh, work),
            (*first, *blocks, tile, x, state),
            [TILE, PARTS, STATE],
            sum(a + b for _, a, b in work),
            [pltpu.VMEM((len(work), COLS, LANES), F32)],
            {at: 0, at + 1: 1, at + 2: 2},
        )

    tile, state = own(1)
    tile, state = own(2)
    work = tuple((offset, 0, 1) for offset in (0, -1, 1, -2, 2))
    tile, x, state = partner(True, work, packed, minus[1], plus[1], minus[2], plus[2])
    tile, x, state = partner(False, ((-3, 1, 1), (3, 1, 1)), minus[3], plus[3])
    tile, state, row_lse = call(
        functools.partial(last_kernel, -4), (x, far, tile, state), [TILE, STATE, ROW_LSE], 2, [pots], {2: 0, 3: 1}
    )
    (col_lse,) = columns(over_plane(row_lse), src_norm, tile, True)
    row_lse = rows(lax.all_to_all(col_lse, "z", 0, 0, tiled=True), tile)
    col_lse, source_pots = columns(over_plane(row_lse), src_norm, tile, False)
    col_lse = joined(lax.all_to_all(col_lse, "z", 0, 0, tiled=True))
    target_pots = (-math.log2(N_SRC) - col_lse) * (1.0 / SCALE) + dst_norm
    return (source_pots.reshape(ROWS), target_pots.reshape(COLS))


def solution(mesh):
    finer = Mesh(mesh.devices.reshape(2, 8, 4, 2, 2), (*BLK, *TGT))
    return jax.shard_map(
        steps,
        mesh=finer,
        in_specs=(P(BLK, None), P((*BLK, *TGT), None), P((*BLK, *TGT))),
        out_specs=(P(BLK), P((*BLK, *TGT))),
        check_vma=False,
    )
```

profile of v0, /device:TPU:1, one launch (start us, length us, event | category | flops | bytes accessed | tf_op | source)
XLA Modules:
  0.0 135.3 jit_solution(12478068734951432763)
XLA Ops:
  0.6 2.1 %collective-permute-start.6 = (f32[1024,128]{1,0:T(8,128)}, f32[1024,128]{1,0:T(8,128)S(1)}, u32[]{:S(2)}, u32[]{:S(2)}) collective-permute-start(f32[1024,128]{1,0:T(8,128)} %sources_ref.1), channel_id=1, source_target_pairs={{0,128},{128,0},{1,129},{129,1},{2,130},{130,2},{3,131},{131,3},{4... | collective-permute-start | bytes 1572872 | tf_op jit(solution)/shard_map/ppermute | solution.py:331
  2.7 0.9 select_maximum_fusion.block_ref.refs_1_
  3.7 5.7 %collective-permute-start = (f32[264,128]{1,0:T(8,128)S(1)}, f32[264,128]{1,0:T(8,128)S(1)}, u32[]{:S(2)}, u32[]{:S(2)}) collective-permute-start(f32[264,128]{1,0:T(8,128)S(1)} %select_maximum_fusion.block_ref.refs_1_), channel_id=1, source_target_pairs={{0,112},{16,32},{32,16},{48,64},{64,48},{80,96},{96,80},{112,0},{1... | collective-permute-start | bytes 405512 | tf_op jit(solution)/shard_map/ppermute | solution.py:336
  9.4 3.0 %collective-permute-done.refs_0_.refs_2_ = f32[264,128]{1,0:T(8,128)S(1)} collective-permute-done((f32[264,128]{1,0:T(8,128)S(1)}, f32[264,128]{1,0:T(8,128)S(1)}, u32[]{:S(2)}, u32[]{:S(2)}) %collective-permute-start) | collective-permute-done | bytes 135200 | tf_op jit(solution)/shard_map/ppermute | solution.py:336
  12.4 1.1 collective-permute-done.3.refs_1_.refs_3_
  13.5 1.3 collective-permute-start.4
  14.9 1.0 copy-done.16
  16.7 1.2 shard_map.51
  18.7 1.6 %shard_map.55 = f32[264,128]{1,0:T(8,128)} custom-call(f32[264,128]{1,0:T(8,128)} %collective-permute-done.1.refs_1_.refs_5_.plus_ref, f32[264,128]{1,0:T(8,128)} %collective-permute-done.4.refs_0_.refs_4_.minus_ref), custom_call_target="tpu_custom_call" | custom-call | bytes 1048576 | tf_op jit(solution)/shard_map/pallas_call | solution.py:184
  20.3 1.5 %collective-permute-start.7 = (f32[264,128]{1,0:T(8,128)}, f32[264,128]{1,0:T(8,128)}, u32[]{:S(2)}, u32[]{:S(2)}) collective-permute-start(f32[264,128]{1,0:T(8,128)} %shard_map.55), channel_id=1, source_target_pairs={{0,32},{1,97},{16,48},{17,113},{32,64},{33,1},{48,80},{49,17},{64,... | collective-permute-start | bytes 405512 | tf_op jit(solution)/shard_map/ppermute | solution.py:206
  23.0 2.2 %shard_map.52 = (f32[8,2,256,1152]{3,2,1,0:T(8,128)S(1)}, f32[2,2,8,1024]{3,2,1,0:T(8,128)S(1)}) custom-call(bf16[2,768,1024]{2,1,0:T(8,128)(2,1)S(1)} %get-tuple-element.21.x_ref.refs_7_, f32[264,128]{1,0:T(8,128)} %collective-permute-done.4.refs_0_.refs_4_.minus_ref, ...), custom_call_target="tpu_custom_call", output_to_operand_aliasing={{0}: (3, {}), {1}: (4, {})} | custom-call | flops 805306368 | bytes 1048576 | tf_op jit(solution)/shard_map/pallas_call | solution.py:184
  25.3 6.4 %copy-done = f32[8,2,256,1152]{3,2,1,0:T(8,128)} copy-done((f32[8,2,256,1152]{3,2,1,0:T(8,128)}, f32[8,2,256,1152]{3,2,1,0:T(8,128)S(1)}, u32[]{:S(2)}) %copy-start) | copy-done | bytes 18874392
  32.5 6.4 %copy-done.1 = f32[8,2,256,1152]{3,2,1,0:T(8,128)S(1)} copy-done((f32[8,2,256,1152]{3,2,1,0:T(8,128)S(1)}, f32[8,2,256,1152]{3,2,1,0:T(8,128)}, u32[]{:S(2)}) %copy-start.1) | copy-done | bytes 18874392
  38.9 1.9 %copy-done.5 = bf16[2,768,1024]{2,1,0:T(8,128)(2,1)S(1)} copy-done((bf16[2,768,1024]{2,1,0:T(8,128)(2,1)S(1)}, bf16[2,768,1024]{2,1,0:T(8,128)(2,1)}, u32[]{:S(2)}) %copy-start.5) | copy-done | bytes 3145752
  40.8 0.9 copy-done.9
  41.7 0.9 copy-done.11
  42.6 0.9 copy-done.13
  43.5 1.0 copy-done.15
  44.5 3.7 %shard_map.53 = (f32[8,2,256,1152]{3,2,1,0:T(8,128)S(1)}, bf16[2,768,1024]{2,1,0:T(8,128)(2,1)S(1)}, f32[2,2,8,1024]{3,2,1,0:T(8,128)S(1)}) custom-call(f32[1024,128]{1,0:T(8,128)S(1)} %copy-done.15, f32[264,128]{1,0:T(8,128)S(1)} %copy-done.13, f32[264,128]{1,0:T(8,128)S(1)} %copy-done.9, ...), custom_call_target="tpu_custom_call", output_to_operand_aliasing={{0}: (6, {}), {1}: (7, {}), {2}: (8, {})} | custom-call | flops 2013265920 | bytes 1048576 | tf_op jit(solution)/shard_map/pallas_call | solution.py:184
  48.2 6.4 %copy-done.2 = f32[8,2,256,1152]{3,2,1,0:T(8,128)} copy-done((f32[8,2,256,1152]{3,2,1,0:T(8,128)}, f32[8,2,256,1152]{3,2,1,0:T(8,128)S(1)}, u32[]{:S(2)}) %copy-start.2) | copy-done | bytes 18874392
  54.7 1.7 %copy-done.6 = bf16[2,768,1024]{2,1,0:T(8,128)(2,1)} copy-done((bf16[2,768,1024]{2,1,0:T(8,128)(2,1)}, bf16[2,768,1024]{2,1,0:T(8,128)(2,1)S(1)}, u32[]{:S(2)}) %copy-start.6) | copy-done | bytes 3145752
  56.4 6.4 %copy-done.3 = f32[8,2,256,1152]{3,2,1,0:T(8,128)S(1)} copy-done((f32[8,2,256,1152]{3,2,1,0:T(8,128)S(1)}, f32[8,2,256,1152]{3,2,1,0:T(8,128)}, u32[]{:S(2)}) %copy-start.3) | copy-done | bytes 18874392
  62.8 1.9 %copy-done.7 = bf16[2,768,1024]{2,1,0:T(8,128)(2,1)S(1)} copy-done((bf16[2,768,1024]{2,1,0:T(8,128)(2,1)S(1)}, bf16[2,768,1024]{2,1,0:T(8,128)(2,1)}, u32[]{:S(2)}) %copy-start.7) | copy-done | bytes 3145752
  64.6 3.1 %shard_map.54 = (f32[8,2,256,1152]{3,2,1,0:T(8,128)S(1)}, bf16[2,768,1024]{2,1,0:T(8,128)(2,1)S(1)}, f32[2,2,8,1024]{3,2,1,0:T(8,128)S(1)}) custom-call(f32[264,128]{1,0:T(8,128)} %collective-permute-done.2.refs_0_, f32[264,128]{1,0:T(8,128)} %collective-permute-done.5.refs_1_, ...), custom_call_target="tpu_custom_call", output_to_operand_aliasing={{0}: (2, {}), {1}: (3, {}), {2}: (4, {})} | custom-call | flops 1610612736 | bytes 1048576 | tf_op jit(solution)/shard_map/pallas_call | solution.py:184
  67.8 2.1 %shard_map.56 = (f32[8,2,256,1152]{3,2,1,0:T(8,128)S(1)}, f32[2,2,8,1024]{3,2,1,0:T(8,128)S(1)}, f32[32,2,8,128]{3,2,1,0:T(8,128)S(1)}) custom-call(bf16[2,768,1024]{2,1,0:T(8,128)(2,1)S(1)} %get-tuple-element.31.x_ref, f32[264,128]{1,0:T(8,128)} %collective-permute-done.7.block_ref, ...), custom_call_target="tpu_custom_call", output_to_operand_aliasing={{0}: (2, {}), {1}: (3, {})} | custom-call | flops 805306368 | bytes 1048576 | tf_op jit(solution)/shard_map/pallas_call | solution.py:184
  69.9 19.7 %all_to_all.20.rows_ref = f32[32,2,8,128]{3,2,1,0:T(8,128)S(1)} all-to-all(f32[32,2,8,128]{3,2,1,0:T(8,128)S(1)} %get-tuple-element.34), channel_id=1, replica_groups=mesh['xl'=2,'z'=8,'y'=4,'xh'=2,'core'=2] {'xl','y','xh','core'}, dimensions={0} | all-to-all | bytes 524288 | tf_op jit(solution)/shard_map/all_to_all | solution.py:340
  89.6 3.3 %shard_map.57 = f32[8,16,128]{2,1,0:T(8,128)S(1)} custom-call(f32[32,2,8,128]{3,2,1,0:T(8,128)S(1)} %all_to_all.20.rows_ref, f32[8,128]{1,0:T(8,128)S(1)} %get-tuple-element.35.src_norm_ref, f32[8,2,256,1152]{3,2,1,0:T(8,128)S(1)} %get-tuple-element.36.tile_ref), custom_call_target="tpu_custom_call" | custom-call | flops 6442450944 | bytes 1048576 | tf_op jit(solution)/shard_map/pallas_call | solution.py:184
  92.9 11.4 %all_to_all.21.cols_ref = f32[8,16,128]{2,1,0:T(8,128)S(1)} all-to-all(f32[8,16,128]{2,1,0:T(8,128)S(1)} %shard_map.57), channel_id=1, replica_groups=mesh['xl'=2,'z'=8,'y'=4,'xh'=2,'core'=2] {'z'}, dimensions={0} | all-to-all | bytes 131072 | tf_op jit(solution)/shard_map/all_to_all | solution.py:387
  104.3 4.2 %shard_map.58 = f32[32,2,8,128]{3,2,1,0:T(8,128)S(1)} custom-call(f32[8,16,128]{2,1,0:T(8,128)S(1)} %all_to_all.21.cols_ref, f32[8,2,256,1152]{3,2,1,0:T(8,128)S(1)} %get-tuple-element.36.tile_ref), custom_call_target="tpu_custom_call" | custom-call | flops 6442450944 | bytes 1048576 | tf_op jit(solution)/shard_map/pallas_call | solution.py:184
  108.4 13.8 %all_to_all.22.rows_ref = f32[32,2,8,128]{3,2,1,0:T(8,128)S(1)} all-to-all(f32[32,2,8,128]{3,2,1,0:T(8,128)S(1)} %shard_map.58), channel_id=1, replica_groups=mesh['xl'=2,'z'=8,'y'=4,'xh'=2,'core'=2] {'xl','y','xh','core'}, dimensions={0} | all-to-all | bytes 524288 | tf_op jit(solution)/shard_map/all_to_all | solution.py:340
  122.3 3.5 %shard_map.59 = (f32[8,2,128]{2,1,0:T(2,128)S(1)}, f32[8,128]{1,0:T(8,128)}) custom-call(f32[32,2,8,128]{3,2,1,0:T(8,128)S(1)} %all_to_all.22.rows_ref, f32[8,128]{1,0:T(8,128)S(1)} %get-tuple-element.35.src_norm_ref, f32[8,2,256,1152]{3,2,1,0:T(8,128)S(1)} %get-tuple-element.36.tile_ref), custom_call_target="tpu_custom_call" | custom-call | flops 6442450944 | bytes 1048576 | tf_op jit(solution)/shard_map/pallas_call | solution.py:184
  125.7 8.9 %all_to_all.23 = f32[8,2,128]{2,1,0:T(2,128)S(1)} all-to-all(f32[8,2,128]{2,1,0:T(2,128)S(1)} %get-tuple-element.38), channel_id=1, replica_groups=mesh['xl'=2,'z'=8,'y'=4,'xh'=2,'core'=2] {'z'}, dimensions={0} | all-to-all | bytes 16384 | tf_op jit(solution)/shard_map/all_to_all | solution.py:389
  (36 shorter events, 4.1 us)
Async XLA Ops:
  0.6 31.1 %collective-permute-start.6 = (f32[1024,128]{1,0:T(8,128)}, f32[1024,128]{1,0:T(8,128)S(1)}, u32[]{:S(2)}, u32[]{:S(2)}) collective-permute-start(f32[1024,128]{1,0:T(8,128)} %sources_ref.1), channel_id=1, source_target_pairs={{0,128},{128,0},{1,129},{129,1},{2,130},{130,2},{3,131},{131,3},{4... | collective-permute-start | bytes 1572872 | tf_op jit(solution)/shard_map/ppermute | solution.py:331
  3.7 21.5 %copy-start.12 = (f32[264,128]{1,0:T(8,128)}, f32[264,128]{1,0:T(8,128)S(1)}, u32[]{:S(2)}) copy-start(f32[264,128]{1,0:T(8,128)S(1)} %select_maximum_fusion.block_ref.refs_1_) | copy-start | bytes 405508
  3.7 8.7 %collective-permute-start = (f32[264,128]{1,0:T(8,128)S(1)}, f32[264,128]{1,0:T(8,128)S(1)}, u32[]{:S(2)}, u32[]{:S(2)}) collective-permute-start(f32[264,128]{1,0:T(8,128)S(1)} %select_maximum_fusion.block_ref.refs_1_), channel_id=1, source_target_pairs={{0,112},{16,32},{32,16},{48,64},{64,48},{80,96},{96,80},{112,0},{1... | collective-permute-start | bytes 405512 | tf_op jit(solution)/shard_map/ppermute | solution.py:336
  9.4 4.2 %collective-permute-start.3 = (f32[264,128]{1,0:T(8,128)S(1)}, f32[264,128]{1,0:T(8,128)S(1)}, u32[]{:S(2)}, u32[]{:S(2)}) collective-permute-start(f32[264,128]{1,0:T(8,128)S(1)} %select_maximum_fusion.block_ref.refs_1_), channel_id=1, source_target_pairs={{0,16},{16,0},{32,48},{48,32},{64,80},{80,64},{96,112},{112,96},{1... | collective-permute-start | bytes 405512 | tf_op jit(solution)/shard_map/ppermute | solution.py:336
  12.4 12.9 %copy-start.8 = (f32[264,128]{1,0:T(8,128)}, f32[264,128]{1,0:T(8,128)S(1)}, u32[]{:S(2)}) copy-start(f32[264,128]{1,0:T(8,128)S(1)} %collective-permute-done.refs_0_.refs_2_) | copy-start | bytes 405508
  12.4 5.6 %collective-permute-start.1 = (f32[264,128]{1,0:T(8,128)S(1)}, f32[264,128]{1,0:T(8,128)}, u32[]{:S(2)}, u32[]{:S(2)}) collective-permute-start(f32[264,128]{1,0:T(8,128)S(1)} %collective-permute-done.refs_0_.refs_2_), channel_id=1, source_target_pairs={{0,16},{16,0},{32,48},{48,32},{64,80},{80,64},{96,112},{112,96},{1... | collective-permute-start | bytes 405512 | tf_op jit(solution)/shard_map/ppermute | solution.py:336
  13.5 11.7 %copy-start.10 = (f32[264,128]{1,0:T(8,128)}, f32[264,128]{1,0:T(8,128)S(1)}, u32[]{:S(2)}) copy-start(f32[264,128]{1,0:T(8,128)S(1)} %collective-permute-done.3.refs_1_.refs_3_) | copy-start | bytes 405508
  13.5 5.2 %collective-permute-start.4 = (f32[264,128]{1,0:T(8,128)S(1)}, f32[264,128]{1,0:T(8,128)}, u32[]{:S(2)}, u32[]{:S(2)}) collective-permute-start(f32[264,128]{1,0:T(8,128)S(1)} %collective-permute-done.3.refs_1_.refs_3_), channel_id=1, source_target_pairs={{0,112},{16,32},{32,16},{48,64},{64,48},{80,96},{96,80},{112,0},{1... | collective-permute-start | bytes 405512 | tf_op jit(solution)/shard_map/ppermute | solution.py:336
  14.9 1.0 copy-start.16
  16.7 8.5 %copy-start.4 = (bf16[2,768,1024]{2,1,0:T(8,128)(2,1)}, bf16[2,768,1024]{2,1,0:T(8,128)(2,1)S(1)}, u32[]{:S(2)}) copy-start(bf16[2,768,1024]{2,1,0:T(8,128)(2,1)S(1)} %get-tuple-element.21.x_ref.refs_7_) | copy-start | bytes 9437188
  20.3 47.4 %collective-permute-start.7 = (f32[264,128]{1,0:T(8,128)}, f32[264,128]{1,0:T(8,128)}, u32[]{:S(2)}, u32[]{:S(2)}) collective-permute-start(f32[264,128]{1,0:T(8,128)} %shard_map.55), channel_id=1, source_target_pairs={{0,32},{1,97},{16,48},{17,113},{32,64},{33,1},{48,80},{49,17},{64,... | collective-permute-start | bytes 405512 | tf_op jit(solution)/shard_map/ppermute | solution.py:206
  21.8 34.5 %collective-permute-start.2 = (f32[264,128]{1,0:T(8,128)}, f32[264,128]{1,0:T(8,128)}, u32[]{:S(2)}, u32[]{:S(2)}) collective-permute-start(f32[264,128]{1,0:T(8,128)} %collective-permute-done.1.refs_1_.refs_5_.plus_ref), channel_id=1, source_target_pairs={{0,112},{16,32},{32,16},{48,64},{64,48},{80,96},{96,80},{112,0},{1... | collective-permute-start | bytes 405512 | tf_op jit(solution)/shard_map/ppermute | solution.py:336
  22.6 33.8 %collective-permute-start.5 = (f32[264,128]{1,0:T(8,128)}, f32[264,128]{1,0:T(8,128)}, u32[]{:S(2)}, u32[]{:S(2)}) collective-permute-start(f32[264,128]{1,0:T(8,128)} %collective-permute-done.4.refs_0_.refs_4_.minus_ref), channel_id=1, source_target_pairs={{0,16},{16,0},{32,48},{48,32},{64,80},{80,64},{96,112},{112,96},{1... | collective-permute-start | bytes 405512 | tf_op jit(solution)/shard_map/ppermute | solution.py:336
  25.2 6.4 %copy-start = (f32[8,2,256,1152]{3,2,1,0:T(8,128)}, f32[8,2,256,1152]{3,2,1,0:T(8,128)S(1)}, u32[]{:S(2)}) copy-start(f32[8,2,256,1152]{3,2,1,0:T(8,128)S(1)} %get-tuple-element.26.refs_6_) | copy-start | bytes 56623108
  31.7 0.8 copy-start.14
  32.5 6.4 %copy-start.1 = (f32[8,2,256,1152]{3,2,1,0:T(8,128)S(1)}, f32[8,2,256,1152]{3,2,1,0:T(8,128)}, u32[]{:S(2)}) copy-start(f32[8,2,256,1152]{3,2,1,0:T(8,128)} %copy-done) | copy-start | bytes 56623108
  38.9 1.9 %copy-start.5 = (bf16[2,768,1024]{2,1,0:T(8,128)(2,1)S(1)}, bf16[2,768,1024]{2,1,0:T(8,128)(2,1)}, u32[]{:S(2)}) copy-start(bf16[2,768,1024]{2,1,0:T(8,128)(2,1)} %copy-done.4) | copy-start | bytes 9437188
  40.7 0.9 copy-start.9
  41.7 0.9 copy-start.11
  42.6 0.9 copy-start.13
  43.5 1.0 copy-start.15
  48.2 6.4 %copy-start.2 = (f32[8,2,256,1152]{3,2,1,0:T(8,128)}, f32[8,2,256,1152]{3,2,1,0:T(8,128)S(1)}, u32[]{:S(2)}) copy-start(f32[8,2,256,1152]{3,2,1,0:T(8,128)S(1)} %get-tuple-element.28.refs_2_) | copy-start | bytes 56623108
  54.7 1.7 %copy-start.6 = (bf16[2,768,1024]{2,1,0:T(8,128)(2,1)}, bf16[2,768,1024]{2,1,0:T(8,128)(2,1)S(1)}, u32[]{:S(2)}) copy-start(bf16[2,768,1024]{2,1,0:T(8,128)(2,1)S(1)} %get-tuple-element.29.refs_3_) | copy-start | bytes 9437188
  56.4 6.4 %copy-start.3 = (f32[8,2,256,1152]{3,2,1,0:T(8,128)S(1)}, f32[8,2,256,1152]{3,2,1,0:T(8,128)}, u32[]{:S(2)}) copy-start(f32[8,2,256,1152]{3,2,1,0:T(8,128)} %copy-done.2) | copy-start | bytes 56623108
  62.8 1.9 %copy-start.7 = (bf16[2,768,1024]{2,1,0:T(8,128)(2,1)S(1)}, bf16[2,768,1024]{2,1,0:T(8,128)(2,1)}, u32[]{:S(2)}) copy-start(bf16[2,768,1024]{2,1,0:T(8,128)(2,1)} %copy-done.6) | copy-start | bytes 9437188
where the time goes:
time: 136 us; the launch traced here: 135 us
  blocking collectives  53.8 us (40%)
  local copies, waits for them, and re-layouts  36.7 us (27%)
  Pallas kernels  25.7 us (19%)
  starting transfers between devices  11.8 us (9%)
  waiting for transfers between devices  4.85 us (4%)
  other arithmetic  1.56 us (1%)
    unnamed x34, local copies, waits for them, and re-layouts  36.7 us
    all_to_all x2, blocking collectives, over_plane(): return lax.all_to_all(copies, PLANE_AXES, 0, 0, tiled=True)  33.5 us
    pallas_call x10, Pallas kernels, call(): pl.pallas_call(kernel, out_shape=outs, in_specs=[VMEM] * len(args), out_s...  25.7 us
    all_to_all x1, blocking collectives, steps(): row_lse = rows(lax.all_to_all(col_lse, 'z', 0, 0, tiled=True), tile)  11.4 us
    all_to_all x1, blocking collectives, steps(): col_lse = joined(lax.all_to_all(col_lse, 'z', 0, 0, tiled=True))  8.93 us
    ppermute x6, starting transfers between devices, swapped(): return lax.ppermute(x, 'z', pairs)  8.15 us
    ppermute x6, waiting for transfers between devices, swapped(): return lax.ppermute(x, 'z', pairs)  4.85 us
  transfers between devices with their start and end apart: 8, of which 3 were waited for; matrix products, arithmetic and copies ran while one was open for 1% of the time, Pallas kernels for 9%

commit v1 on v0

--- a/solution.py
+++ b/solution.py
@@ -174,7 +174,7 @@
 
 
 F32 = jnp.float32
-TILE = jax.ShapeDtypeStruct((RING, 2, COLS, ROWS + LANES), F32)
+TILE = jax.ShapeDtypeStruct((RING, 2, COLS, ROWS), F32)
 PARTS = jax.ShapeDtypeStruct((2, 6 * LANES, ROWS), jnp.bfloat16)
 STATE = jax.ShapeDtypeStruct((2, 2, 8, ROWS), F32)
 ROW_LSE = jax.ShapeDtypeStruct((PLANE, 2, TILES, LANES), F32)
@@ -274,54 +274,45 @@
 
 def rows_kernel(cols_ref, tile_ref, rows_ref, w_scr, pots_scr, high_scr, total_scr):
     eye = diagonal()
-    w = -math.log2(N_SRC) - joined(cols_ref[...])
-    for r in range(2 * RING):
-        w_scr[r] = w[r : r + 1, :]
+    w_scr[...] = (-math.log2(N_SRC) - joined(cols_ref[...])).reshape(RING, 2, LANES)
     high_scr[...] = jnp.full_like(high_scr, -3.0e38)
     total_scr[...] = jnp.zeros_like(total_scr)
-    unit = 8
-    count = COLS // 8 // unit
-
-    def spread(k):
+
+    def spread(k, slot):
         for c in range(2):
-            pots_scr[k, c * LANES : (c + 1) * LANES, :] = jnp.broadcast_to(as_column(eye, w_scr[2 * k + c]), (LANES, LANES))
-
-    def load(k, tile, part):
-        half, t = divmod(tile, TILES)
-        lanes = slice(t * LANES, (t + 1) * LANES)
-        rows = [slice(8 * r, 8 * r + 8) for r in range(part * unit, (part + 1) * unit)]
-        scores = [tile_ref[k, half, r, lanes] + pots_scr[k, r, :] for r in rows]
-        return tree(jnp.maximum, scores), scores
-
-    def body(k, held):
-        for tile in range(2 * TILES):
-            before, total = high_scr[tile], total_scr[tile]
-            for part in range(count):
-                if part + 1 < count:
-                    following = load(k, tile, part + 1)
-                elif tile + 1 < 2 * TILES:
-                    following = load(k, tile + 1, 0)
-                else:
-                    following = load(jnp.minimum(k + 1, RING - 1), 0, 0)
-                high, scores = jnp.maximum(held[0], before), held[1]
-                total = total * jnp.exp2(before - high) + tree(jnp.add, [jnp.exp2(s - high) for s in scores])
-                before, held = high, following
-            high_scr[tile], total_scr[tile] = before, total
-        spread(jnp.minimum(k + 2, RING - 1))
-        return held
-
-    spread(0)
-    spread(1)
-    lax.fori_loop(0, RING, body, load(0, 0, 0))
-    put_rows(rows_ref, lambda half, tile: (high_scr[half * TILES + tile], total_scr[half * TILES + tile]))
+            column = as_column(eye, w_scr[k, c : c + 1, :])
+            pots_scr[slot, c * LANES : (c + 1) * LANES, :] = jnp.broadcast_to(column, (LANES, LANES))
+
+    def block(k, slot):
+        for half in range(2):
+            for t in range(TILES):
+                tile = slice(t * LANES, (t + 1) * LANES)
+                state = high_scr[half, :, tile], total_scr[half, :, tile]
+                for c in range(0, COLS, 64):
+                    rows = range(c, c + 64, 8)
+                    scores = [tile_ref[k, half, r : r + 8, tile] + pots_scr[slot, r : r + 8, :] for r in rows]
+                    state = online(scores, state)
+                high_scr[half, :, tile], total_scr[half, :, tile] = state
+
+    def two_blocks(i, carry):
+        spread(2 * i + 1, 1)
+        block(2 * i, 0)
+        spread(jnp.minimum(2 * i + 2, RING - 1), 0)
+        block(2 * i + 1, 1)
+        return carry
+
+    spread(0, 0)
+    lax.fori_loop(0, RING // 2, two_blocks, 0)
+    tiles = [slice(t * LANES, (t + 1) * LANES) for t in range(TILES)]
+    put_rows(rows_ref, lambda half, t: (high_scr[half, :, tiles[t]], total_scr[half, :, tiles[t]]))
 
 
 def rows(cols, tile):
     scratch = [
-        pltpu.VMEM((2 * RING, 1, LANES), F32),
-        pltpu.VMEM((RING, COLS, LANES), F32),
-        pltpu.VMEM((2 * TILES, 8, LANES), F32),
-        pltpu.VMEM((2 * TILES, 8, LANES), F32),
+        pltpu.VMEM((RING, 2, LANES), F32),
+        pltpu.VMEM((2, COLS, LANES), F32),
+        pltpu.VMEM((2, 8, ROWS), F32),
+        pltpu.VMEM((2, 8, ROWS), F32),
     ]
     return call(rows_kernel, (cols, tile), [ROW_LSE], 16, scratch)[0]
 
@@ -376,8 +367,7 @@
         )
 
     tile, state = own(1)
-    tile, state = own(2)
-    work = tuple((offset, 0, 1) for offset in (0, -1, 1, -2, 2))
+    work = ((0, 0, 1), (-1, 0, 1), (1, 0, 1), (-2, 1, 1), (2, 1, 1))
     tile, x, state = partner(True, work, packed, minus[1], plus[1], minus[2], plus[2])
     tile, x, state = partner(False, ((-3, 1, 1), (3, 1, 1)), minus[3], plus[3])
     tile, state, row_lse = call(

time: 136 us -> 94.9 us (0.70)
  local copies, waits for them, and re-layouts: 36.7 us -> 1.04 us
  Pallas kernels: 25.7 us -> 19.8 us
  waiting for transfers between devices: 4.85 us -> 6.24 us
    unnamed x34 -> x2, local copies, waits for them, and re-layouts: 36.7 us -> 1.04 us
    pallas_call x10 -> x9, Pallas kernels: 25.7 us -> 19.8 us  [call(): pl.pallas_call(kernel, out_shape=outs, in_specs=[VMEM] * len(args), out_s...]
    ppermute x6, waiting for transfers between devices: 4.85 us -> 6.23 us  [swapped(): return lax.ppermute(x, 'z', pairs)]
  transfers between devices with their start and end apart: 8 -> 8, of which waited for: 3 -> 5; matrix products, arithmetic and copies ran while one was open for 1% -> 1% of each run, Pallas kernels for 9% -> 8%
where the time goes in v1:
time: 94.9 us; the launch traced here: 94.7 us
  blocking collectives  53.5 us (56%)
  Pallas kernels  19.8 us (21%)
  starting transfers between devices  11.8 us (12%)
  waiting for transfers between devices  6.24 us (7%)
  other arithmetic  1.56 us (2%)
  local copies, waits for them, and re-layouts  1.04 us (1%)
    all_to_all x2, blocking collectives, over_plane(): return lax.all_to_all(copies, PLANE_AXES, 0, 0, tiled=True)  32.8 us
    pallas_call x9, Pallas kernels, call(): pl.pallas_call(kernel, out_shape=outs, in_specs=[VMEM] * len(args), out_s...  19.8 us
    all_to_all x1, blocking collectives, steps(): row_lse = rows(lax.all_to_all(col_lse, 'z', 0, 0, tiled=True), tile)  11.8 us
    all_to_all x1, blocking collectives, steps(): col_lse = joined(lax.all_to_all(col_lse, 'z', 0, 0, tiled=True))  8.93 us
    ppermute x6, starting transfers between devices, swapped(): return lax.ppermute(x, 'z', pairs)  8.05 us
    ppermute x6, waiting for transfers between devices, swapped(): return lax.ppermute(x, 'z', pairs)  6.23 us
    ppermute x1, starting transfers between devices, shifted(): return lax.ppermute(x, axis, [(i, (i + by) % count) for i in range(count)])  2.12 us
  transfers between devices with their start and end apart: 8, of which 5 were waited for; matrix products, arithmetic and copies ran while one was open for 1% of the time, Pallas kernels for 8%

profile of v1, /device:TPU:1, one launch (start us, length us, event | category | flops | bytes accessed | tf_op | source)
XLA Modules:
  0.0 94.7 jit_solution(3085039615794986845)
XLA Ops:
  0.6 2.1 %collective-permute-start.6 = (f32[1024,128]{1,0:T(8,128)}, f32[1024,128]{1,0:T(8,128)S(1)}, u32[]{:S(2)}, u32[]{:S(2)}) collective-permute-start(f32[1024,128]{1,0:T(8,128)} %sources_ref.1), channel_id=1, source_target_pairs={{0,128},{128,0},{1,129},{129,1},{2,130},{130,2},{3,131},{131,3},{4... | collective-permute-start | bytes 1572872 | tf_op jit(solution)/shard_map/ppermute | solution.py:322
  2.7 0.9 select_maximum_fusion.block_ref.refs_1_
  3.7 5.7 %collective-permute-start = (f32[264,128]{1,0:T(8,128)S(1)}, f32[264,128]{1,0:T(8,128)S(1)}, u32[]{:S(2)}, u32[]{:S(2)}) collective-permute-start(f32[264,128]{1,0:T(8,128)S(1)} %select_maximum_fusion.block_ref.refs_1_), channel_id=1, source_target_pairs={{0,112},{16,32},{32,16},{48,64},{64,48},{80,96},{96,80},{112,0},{1... | collective-permute-start | bytes 405512 | tf_op jit(solution)/shard_map/ppermute | solution.py:327
  9.3 0.0 collective-permute-start.3
  9.3 3.0 %collective-permute-done.refs_0_.refs_2_ = f32[264,128]{1,0:T(8,128)S(1)} collective-permute-done((f32[264,128]{1,0:T(8,128)S(1)}, f32[264,128]{1,0:T(8,128)S(1)}, u32[]{:S(2)}, u32[]{:S(2)}) %collective-permute-start) | collective-permute-done | bytes 135200 | tf_op jit(solution)/shard_map/ppermute | solution.py:327
  12.4 0.0 collective-permute-start.1
  12.4 1.1 %collective-permute-done.3.refs_1_.refs_3_ = f32[264,128]{1,0:T(8,128)S(1)} collective-permute-done((f32[264,128]{1,0:T(8,128)S(1)}, f32[264,128]{1,0:T(8,128)S(1)}, u32[]{:S(2)}, u32[]{:S(2)}) %collective-permute-start.3) | collective-permute-done | bytes 135200 | tf_op jit(solution)/shard_map/ppermute | solution.py:327
  13.5 1.3 %collective-permute-start.4 = (f32[264,128]{1,0:T(8,128)S(1)}, f32[264,128]{1,0:T(8,128)S(1)}, u32[]{:S(2)}, u32[]{:S(2)}) collective-permute-start(f32[264,128]{1,0:T(8,128)S(1)} %collective-permute-done.3.refs_1_.refs_3_), channel_id=1, source_target_pairs={{0,112},{16,32},{32,16},{48,64},{64,48},{80,96},{96,80},{112,0},{1... | collective-permute-start | bytes 405512 | tf_op jit(solution)/shard_map/ppermute | solution.py:327
  14.8 0.0 copy-start
  14.8 1.0 %copy-done = f32[1024,128]{1,0:T(8,128)S(1)} copy-done((f32[1024,128]{1,0:T(8,128)S(1)}, f32[1024,128]{1,0:T(8,128)}, u32[]{:S(2)}) %copy-start) | copy-done | bytes 524312
  15.8 0.8 shard_map.50
  16.6 1.2 %shard_map.51 = (f32[8,2,256,1024]{3,2,1,0:T(8,128)S(1)}, f32[2,2,8,1024]{3,2,1,0:T(8,128)S(1)}) custom-call(bf16[2,768,1024]{2,1,0:T(8,128)(2,1)S(1)} %get-tuple-element.19.x_ref.refs_7_, f32[264,128]{1,0:T(8,128)S(1)} %collective-permute-done.refs_0_.refs_2_, ...), custom_call_target="tpu_custom_call", output_to_operand_aliasing={{0}: (3, {}), {1}: (4, {})} | custom-call | flops 805306368 | bytes 1048576 | tf_op jit(solution)/shard_map/pallas_call | solution.py:184
  17.9 0.0 collective-permute-done.1.refs_5_.plus_ref
  17.9 0.7 collective-permute-done.4.refs_4_.minus_ref
  18.6 1.6 %collective-permute-start.7 = (f32[264,128]{1,0:T(8,128)S(1)}, f32[264,128]{1,0:T(8,128)S(1)}, u32[]{:S(2)}, u32[]{:S(2)}) collective-permute-start(f32[264,128]{1,0:T(8,128)S(1)} %shard_map.54), channel_id=1, source_target_pairs={{0,32},{1,97},{16,48},{17,113},{32,64},{33,1},{48,80},{49,17},{64,... | collective-permute-start | bytes 405512 | tf_op jit(solution)/shard_map/ppermute | solution.py:206
  20.2 0.7 collective-permute-start.2
  20.9 0.4 collective-permute-start.5
  21.3 0.0 collective-permute-done.6.refs_0_
  21.3 3.7 %shard_map.52 = (f32[8,2,256,1024]{3,2,1,0:T(8,128)S(1)}, bf16[2,768,1024]{2,1,0:T(8,128)(2,1)S(1)}, f32[2,2,8,1024]{3,2,1,0:T(8,128)S(1)}) custom-call(f32[1024,128]{1,0:T(8,128)S(1)} %collective-permute-done.6.refs_0_, f32[264,128]{1,0:T(8,128)S(1)} %select_maximum_fusion.block_ref.refs_1_, ...), custom_call_target="tpu_custom_call", output_to_operand_aliasing={{0}: (6, {}), {1}: (7, {}), {2}: (8, {})} | custom-call | flops 2818572288 | bytes 1048576 | tf_op jit(solution)/shard_map/pallas_call | solution.py:184
  25.0 1.0 %collective-permute-done.2.refs_0_ = f32[264,128]{1,0:T(8,128)S(1)} collective-permute-done((f32[264,128]{1,0:T(8,128)S(1)}, f32[264,128]{1,0:T(8,128)S(1)}, u32[]{:S(2)}, u32[]{:S(2)}) %collective-permute-start.2) | collective-permute-done | bytes 135200 | tf_op jit(solution)/shard_map/ppermute | solution.py:327
  26.0 0.4 collective-permute-done.5.refs_1_
  26.4 2.2 %shard_map.53 = (f32[8,2,256,1024]{3,2,1,0:T(8,128)S(1)}, bf16[2,768,1024]{2,1,0:T(8,128)(2,1)S(1)}, f32[2,2,8,1024]{3,2,1,0:T(8,128)S(1)}) custom-call(f32[264,128]{1,0:T(8,128)S(1)} %collective-permute-done.2.refs_0_, f32[264,128]{1,0:T(8,128)S(1)} %collective-permute-done.5.refs_1_, ...), custom_call_target="tpu_custom_call", output_to_operand_aliasing={{0}: (2, {}), {1}: (3, {}), {2}: (4, {})} | custom-call | flops 1610612736 | bytes 1048576 | tf_op jit(solution)/shard_map/pallas_call | solution.py:184
  28.6 0.0 collective-permute-done.7.block_ref
  28.6 1.2 %shard_map.55 = (f32[8,2,256,1024]{3,2,1,0:T(8,128)S(1)}, f32[2,2,8,1024]{3,2,1,0:T(8,128)S(1)}, f32[32,2,8,128]{3,2,1,0:T(8,128)S(1)}) custom-call(bf16[2,768,1024]{2,1,0:T(8,128)(2,1)S(1)} %get-tuple-element.27.x_ref, f32[264,128]{1,0:T(8,128)S(1)} %collective-permute-done.7.block_ref, ...), custom_call_target="tpu_custom_call", output_to_operand_aliasing={{0}: (2, {}), {1}: (3, {})} | custom-call | flops 805306368 | bytes 1048576 | tf_op jit(solution)/shard_map/pallas_call | solution.py:184
  29.9 18.9 %all_to_all.20.rows_ref = f32[32,2,8,128]{3,2,1,0:T(8,128)S(1)} all-to-all(f32[32,2,8,128]{3,2,1,0:T(8,128)S(1)} %get-tuple-element.30), channel_id=1, replica_groups=mesh['xl'=2,'z'=8,'y'=4,'xh'=2,'core'=2] {'xl','y','xh','core'}, dimensions={0} | all-to-all | bytes 524288 | tf_op jit(solution)/shard_map/all_to_all | solution.py:331
  48.8 3.3 %shard_map.56 = f32[8,16,128]{2,1,0:T(8,128)S(1)} custom-call(f32[32,2,8,128]{3,2,1,0:T(8,128)S(1)} %all_to_all.20.rows_ref, f32[8,128]{1,0:T(8,128)S(1)} %get-tuple-element.31.src_norm_ref, f32[8,2,256,1024]{3,2,1,0:T(8,128)S(1)} %get-tuple-element.32.tile_ref), custom_call_target="tpu_custom_call" | custom-call | flops 6442450944 | bytes 1048576 | tf_op jit(solution)/shard_map/pallas_call | solution.py:184
  52.1 11.8 %all_to_all.21.cols_ref = f32[8,16,128]{2,1,0:T(8,128)S(1)} all-to-all(f32[8,16,128]{2,1,0:T(8,128)S(1)} %shard_map.56), channel_id=1, replica_groups=mesh['xl'=2,'z'=8,'y'=4,'xh'=2,'core'=2] {'z'}, dimensions={0} | all-to-all | bytes 131072 | tf_op jit(solution)/shard_map/all_to_all | solution.py:377
  64.0 3.8 %shard_map.57 = f32[32,2,8,128]{3,2,1,0:T(8,128)S(1)} custom-call(f32[8,16,128]{2,1,0:T(8,128)S(1)} %all_to_all.21.cols_ref, f32[8,2,256,1024]{3,2,1,0:T(8,128)S(1)} %get-tuple-element.32.tile_ref), custom_call_target="tpu_custom_call" | custom-call | flops 6442450944 | bytes 1048576 | tf_op jit(solution)/shard_map/pallas_call | solution.py:184
  67.8 13.8 %all_to_all.22.rows_ref = f32[32,2,8,128]{3,2,1,0:T(8,128)S(1)} all-to-all(f32[32,2,8,128]{3,2,1,0:T(8,128)S(1)} %shard_map.57), channel_id=1, replica_groups=mesh['xl'=2,'z'=8,'y'=4,'xh'=2,'core'=2] {'xl','y','xh','core'}, dimensions={0} | all-to-all | bytes 524288 | tf_op jit(solution)/shard_map/all_to_all | solution.py:331
  81.6 3.5 %shard_map.58 = (f32[8,2,128]{2,1,0:T(2,128)S(1)}, f32[8,128]{1,0:T(8,128)}) custom-call(f32[32,2,8,128]{3,2,1,0:T(8,128)S(1)} %all_to_all.22.rows_ref, f32[8,128]{1,0:T(8,128)S(1)} %get-tuple-element.31.src_norm_ref, f32[8,2,256,1024]{3,2,1,0:T(8,128)S(1)} %get-tuple-element.32.tile_ref), custom_call_target="tpu_custom_call" | custom-call | flops 6442450944 | bytes 1048576 | tf_op jit(solution)/shard_map/pallas_call | solution.py:184
  85.1 8.9 %all_to_all.23 = f32[8,2,128]{2,1,0:T(2,128)S(1)} all-to-all(f32[8,2,128]{2,1,0:T(2,128)S(1)} %get-tuple-element.34), channel_id=1, replica_groups=mesh['xl'=2,'z'=8,'y'=4,'xh'=2,'core'=2] {'z'}, dimensions={0} | all-to-all | bytes 16384 | tf_op jit(solution)/shard_map/all_to_all | solution.py:379
  94.1 0.6 add_bitcast_fusion
  (3 shorter events, 0.1 us)
Async XLA Ops:
  0.6 20.7 %collective-permute-start.6 = (f32[1024,128]{1,0:T(8,128)}, f32[1024,128]{1,0:T(8,128)S(1)}, u32[]{:S(2)}, u32[]{:S(2)}) collective-permute-start(f32[1024,128]{1,0:T(8,128)} %sources_ref.1), channel_id=1, source_target_pairs={{0,128},{128,0},{1,129},{129,1},{2,130},{130,2},{3,131},{131,3},{4... | collective-permute-start | bytes 1572872 | tf_op jit(solution)/shard_map/ppermute | solution.py:322
  3.7 8.7 %collective-permute-start = (f32[264,128]{1,0:T(8,128)S(1)}, f32[264,128]{1,0:T(8,128)S(1)}, u32[]{:S(2)}, u32[]{:S(2)}) collective-permute-start(f32[264,128]{1,0:T(8,128)S(1)} %select_maximum_fusion.block_ref.refs_1_), channel_id=1, source_target_pairs={{0,112},{16,32},{32,16},{48,64},{64,48},{80,96},{96,80},{112,0},{1... | collective-permute-start | bytes 405512 | tf_op jit(solution)/shard_map/ppermute | solution.py:327
  9.3 4.2 %collective-permute-start.3 = (f32[264,128]{1,0:T(8,128)S(1)}, f32[264,128]{1,0:T(8,128)S(1)}, u32[]{:S(2)}, u32[]{:S(2)}) collective-permute-start(f32[264,128]{1,0:T(8,128)S(1)} %select_maximum_fusion.block_ref.refs_1_), channel_id=1, source_target_pairs={{0,16},{16,0},{32,48},{48,32},{64,80},{80,64},{96,112},{112,96},{1... | collective-permute-start | bytes 405512 | tf_op jit(solution)/shard_map/ppermute | solution.py:327
  12.4 5.5 %collective-permute-start.1 = (f32[264,128]{1,0:T(8,128)S(1)}, f32[264,128]{1,0:T(8,128)S(1)}, u32[]{:S(2)}, u32[]{:S(2)}) collective-permute-start(f32[264,128]{1,0:T(8,128)S(1)} %collective-permute-done.refs_0_.refs_2_), channel_id=1, source_target_pairs={{0,16},{16,0},{32,48},{48,32},{64,80},{80,64},{96,112},{112,96},{1... | collective-permute-start | bytes 405512 | tf_op jit(solution)/shard_map/ppermute | solution.py:327
  13.5 5.1 %collective-permute-start.4 = (f32[264,128]{1,0:T(8,128)S(1)}, f32[264,128]{1,0:T(8,128)S(1)}, u32[]{:S(2)}, u32[]{:S(2)}) collective-permute-start(f32[264,128]{1,0:T(8,128)S(1)} %collective-permute-done.3.refs_1_.refs_3_), channel_id=1, source_target_pairs={{0,112},{16,32},{32,16},{48,64},{64,48},{80,96},{96,80},{112,0},{1... | collective-permute-start | bytes 405512 | tf_op jit(solution)/shard_map/ppermute | solution.py:327
  14.8 1.0 %copy-start = (f32[1024,128]{1,0:T(8,128)S(1)}, f32[1024,128]{1,0:T(8,128)}, u32[]{:S(2)}) copy-start(f32[1024,128]{1,0:T(8,128)} %sources_ref.1) | copy-start | bytes 1572868
  18.6 10.0 %collective-permute-start.7 = (f32[264,128]{1,0:T(8,128)S(1)}, f32[264,128]{1,0:T(8,128)S(1)}, u32[]{:S(2)}, u32[]{:S(2)}) collective-permute-start(f32[264,128]{1,0:T(8,128)S(1)} %shard_map.54), channel_id=1, source_target_pairs={{0,32},{1,97},{16,48},{17,113},{32,64},{33,1},{48,80},{49,17},{64,... | collective-permute-start | bytes 405512 | tf_op jit(solution)/shard_map/ppermute | solution.py:206
  20.2 5.8 %collective-permute-start.2 = (f32[264,128]{1,0:T(8,128)S(1)}, f32[264,128]{1,0:T(8,128)S(1)}, u32[]{:S(2)}, u32[]{:S(2)}) collective-permute-start(f32[264,128]{1,0:T(8,128)S(1)} %collective-permute-done.1.refs_5_.plus_ref), channel_id=1, source_target_pairs={{0,112},{16,32},{32,16},{48,64},{64,48},{80,96},{96,80},{112,0},{1... | collective-permute-start | bytes 405512 | tf_op jit(solution)/shard_map/ppermute | solution.py:327
  20.9 5.5 %collective-permute-start.5 = (f32[264,128]{1,0:T(8,128)S(1)}, f32[264,128]{1,0:T(8,128)S(1)}, u32[]{:S(2)}, u32[]{:S(2)}) collective-permute-start(f32[264,128]{1,0:T(8,128)S(1)} %collective-permute-done.4.refs_4_.minus_ref), channel_id=1, source_target_pairs={{0,16},{16,0},{32,48},{48,32},{64,80},{80,64},{96,112},{112,96},{1... | collective-permute-start | bytes 405512 | tf_op jit(solution)/shard_map/ppermute | solution.py:327

commit v2 on v1

--- a/solution.py
+++ b/solution.py
@@ -138,30 +138,39 @@
     add_block(parts, pots_scr, z, mine, x_ref, tile_ref, state_ref, True)
 
 
-def own_kernel(offsets, x_ref, *refs):
-    blocks, (tile_ref, state_ref), pots_scr = refs[: len(offsets)], refs[-3:-1], refs[-1]
+def own_kernel(x_ref, packed_ref, minus_ref, plus_ref, *refs):
+    tile_ref, state_ref, kept_ref, pots_ref = refs[2:]
     z, mine = lax.axis_index("z"), lax.axis_index("xl")
     eye = diagonal()
-    for b, offset in enumerate(offsets):
-        parts, _ = prepare_targets(eye, blocks[b], pots_scr.at[b])
-        add_block(parts, pots_scr.at[b], ring_index(z, offset), mine, x_ref, tile_ref, state_ref, False)
+    for b, (block_ref, offset) in enumerate(((packed_ref, 0), (minus_ref, -1), (plus_ref, 1))):
+        parts, _ = prepare_targets(eye, block_ref, pots_ref.at[b])
+        kept_ref[b] = parts
+        if offset:
+            add_block(parts, pots_ref.at[b], ring_index(z, offset), mine, x_ref, tile_ref, state_ref, False)
 
 
 def partner_kernel(fresh, work, *refs):
     refs = list(refs)
-    sources_ref = refs.pop(0) if fresh else None
-    blocks, (tile_ref, x_ref, state_ref), pots_scr = refs[: len(work)], refs[-4:-1], refs[-1]
+    ready = 0
+    if fresh:
+        sources_ref, kept_ref, kept_pots_ref = refs.pop(0), refs.pop(0), refs.pop(0)
+        ready = kept_ref.shape[0]
+    blocks, (tile_ref, x_ref, state_ref), pots_scr = refs[: len(work) - ready], refs[-4:-1], refs[-1]
     z, mine = lax.axis_index("z"), lax.axis_index("xl")
     eye = diagonal()
     if fresh:
         prepare_sources(sources_ref[...], 1 - mine, x_ref)
     for b, (offset, own, partner) in enumerate(work):
-        parts, _ = prepare_targets(eye, blocks[b], pots_scr.at[b])
+        if b < ready:
+            parts, pots_ref = kept_ref[b], kept_pots_ref.at[b]
+        else:
+            pots_ref = pots_scr.at[b]
+            parts, _ = prepare_targets(eye, blocks[b - ready], pots_ref)
         at = ring_index(z, offset)
         if own:
-            add_block(parts, pots_scr.at[b], at, mine, x_ref, tile_ref, state_ref, False)
+            add_block(parts, pots_ref, at, mine, x_ref, tile_ref, state_ref, False)
         if partner:
-            add_block(parts, pots_scr.at[b], at, 1 - mine, x_ref, tile_ref, state_ref, fresh and b == 0)
+            add_block(parts, pots_ref, at, 1 - mine, x_ref, tile_ref, state_ref, fresh and b == 0)
 
 
 def last_kernel(offset, x_ref, block_ref, *refs):
@@ -343,19 +352,13 @@
     pots = pltpu.VMEM((COLS, LANES), F32)
     norms = [jax.ShapeDtypeStruct((TILES, LANES), F32), jax.ShapeDtypeStruct((2, LANES), F32)]
     tile, x, state, src_norm, dst_norm = call(start_kernel, (sources, packed), [TILE, PARTS, STATE, *norms], 1, [pots])
-
-    def own(step):
-        return call(
-            functools.partial(own_kernel, (-step, step)),
-            (x, minus[step], plus[step], tile, state),
-            [TILE, STATE],
-            2,
-            [pltpu.VMEM((2, COLS, LANES), F32)],
-            {3: 0, 4: 1},
-        )
+    kept = [jax.ShapeDtypeStruct((3, COLS, 6 * LANES), jnp.bfloat16), jax.ShapeDtypeStruct((3, COLS, LANES), F32)]
+    tile, state, *kept = call(
+        own_kernel, (x, packed, minus[1], plus[1], tile, state), [TILE, STATE, *kept], 2, (), {4: 0, 5: 1}
+    )
 
     def partner(fresh, work, *blocks):
-        first = (others,) if fresh else ()
+        first = (others, *kept) if fresh else ()
         at = len(first) + len(blocks)
         return call(
             functools.partial(partner_kernel, fresh, work),
@@ -366,9 +369,8 @@
             {at: 0, at + 1: 1, at + 2: 2},
         )
 
-    tile, state = own(1)
     work = ((0, 0, 1), (-1, 0, 1), (1, 0, 1), (-2, 1, 1), (2, 1, 1))
-    tile, x, state = partner(True, work, packed, minus[1], plus[1], minus[2], plus[2])
+    tile, x, state = partner(True, work, minus[2], plus[2])
     tile, x, state = partner(False, ((-3, 1, 1), (3, 1, 1)), minus[3], plus[3])
     tile, state, row_lse = call(
         functools.partial(last_kernel, -4), (x, far, tile, state), [TILE, STATE, ROW_LSE], 2, [pots], {2: 0, 3: 1}

time: 94.9 us -> 95 us (level)
  no operation moved by 1% of the time
where the time goes in v2:
time: 95 us; the launch traced here: 94.7 us
  blocking collectives  53.5 us (56%)
  Pallas kernels  19.8 us (21%)
  starting transfers between devices  11.8 us (12%)
  waiting for transfers between devices  6.26 us (7%)
  other arithmetic  1.56 us (2%)
  local copies, waits for them, and re-layouts  1.04 us (1%)
    all_to_all x2, blocking collectives, over_plane(): return lax.all_to_all(copies, PLANE_AXES, 0, 0, tiled=True)  32.7 us
    pallas_call x9, Pallas kernels, call(): pl.pallas_call(kernel, out_shape=outs, in_specs=[VMEM] * len(args), out_s...  19.8 us
    all_to_all x1, blocking collectives, steps(): row_lse = rows(lax.all_to_all(col_lse, 'z', 0, 0, tiled=True), tile)  11.8 us
    all_to_all x1, blocking collectives, steps(): col_lse = joined(lax.all_to_all(col_lse, 'z', 0, 0, tiled=True))  8.93 us
    ppermute x6, starting transfers between devices, swapped(): return lax.ppermute(x, 'z', pairs)  8.05 us
    ppermute x6, waiting for transfers between devices, swapped(): return lax.ppermute(x, 'z', pairs)  6.25 us
    ppermute x1, starting transfers between devices, shifted(): return lax.ppermute(x, axis, [(i, (i + by) % count) for i in range(count)])  2.12 us
  transfers between devices with their start and end apart: 8, of which 5 were waited for; matrix products, arithmetic and copies ran while one was open for 1% of the time, Pallas kernels for 8%

profile of v2, /device:TPU:1, one launch (start us, length us, event | category | flops | bytes accessed | tf_op | source)
XLA Modules:
  0.0 94.7 jit_solution(4234495832440957771)
XLA Ops:
  0.6 2.1 %collective-permute-start.6 = (f32[1024,128]{1,0:T(8,128)}, f32[1024,128]{1,0:T(8,128)S(1)}, u32[]{:S(2)}, u32[]{:S(2)}) collective-permute-start(f32[1024,128]{1,0:T(8,128)} %sources_ref.1), channel_id=1, source_target_pairs={{0,128},{128,0},{1,129},{129,1},{2,130},{130,2},{3,131},{131,3},{4... | collective-permute-start | bytes 1572872 | tf_op jit(solution)/shard_map/ppermute | solution.py:331
  2.7 0.9 select_maximum_fusion.block_ref.packed_ref
  3.7 5.7 %collective-permute-start = (f32[264,128]{1,0:T(8,128)S(1)}, f32[264,128]{1,0:T(8,128)S(1)}, u32[]{:S(2)}, u32[]{:S(2)}) collective-permute-start(f32[264,128]{1,0:T(8,128)S(1)} %select_maximum_fusion.block_ref.packed_ref), channel_id=1, source_target_pairs={{0,112},{16,32},{32,16},{48,64},{64,48},{80,96},{96,80},{112,0},{1... | collective-permute-start | bytes 405512 | tf_op jit(solution)/shard_map/ppermute | solution.py:336
  9.3 0.0 collective-permute-start.3
  9.3 3.0 %collective-permute-done.minus_ref = f32[264,128]{1,0:T(8,128)S(1)} collective-permute-done((f32[264,128]{1,0:T(8,128)S(1)}, f32[264,128]{1,0:T(8,128)S(1)}, u32[]{:S(2)}, u32[]{:S(2)}) %collective-permute-start) | collective-permute-done | bytes 135200 | tf_op jit(solution)/shard_map/ppermute | solution.py:336
  12.4 0.0 collective-permute-start.1
  12.4 1.1 %collective-permute-done.3.plus_ref = f32[264,128]{1,0:T(8,128)S(1)} collective-permute-done((f32[264,128]{1,0:T(8,128)S(1)}, f32[264,128]{1,0:T(8,128)S(1)}, u32[]{:S(2)}, u32[]{:S(2)}) %collective-permute-start.3) | collective-permute-done | bytes 135200 | tf_op jit(solution)/shard_map/ppermute | solution.py:336
  13.5 1.3 %collective-permute-start.4 = (f32[264,128]{1,0:T(8,128)S(1)}, f32[264,128]{1,0:T(8,128)S(1)}, u32[]{:S(2)}, u32[]{:S(2)}) collective-permute-start(f32[264,128]{1,0:T(8,128)S(1)} %collective-permute-done.3.plus_ref), channel_id=1, source_target_pairs={{0,112},{16,32},{32,16},{48,64},{64,48},{80,96},{96,80},{112,0},{1... | collective-permute-start | bytes 405512 | tf_op jit(solution)/shard_map/ppermute | solution.py:336
  14.8 0.0 copy-start
  14.8 1.0 %copy-done = f32[1024,128]{1,0:T(8,128)S(1)} copy-done((f32[1024,128]{1,0:T(8,128)S(1)}, f32[1024,128]{1,0:T(8,128)}, u32[]{:S(2)}) %copy-start) | copy-done | bytes 524312
  15.8 0.8 shard_map.50
  16.6 1.2 %shard_map.51 = (f32[8,2,256,1024]{3,2,1,0:T(8,128)S(1)}, f32[2,2,8,1024]{3,2,1,0:T(8,128)S(1)}, bf16[3,256,768]{2,1,0:T(8,128)(2,1)S(1)}, f32[3,256,128]{2,1,0:T(8,128)S(1)}) custom-call(bf16[2,768,1024]{2,1,0:T(8,128)(2,1)S(1)} %get-tuple-element.21.x_ref.refs_6_, ...), custom_call_target="tpu_custom_call", output_to_operand_aliasing={{0}: (4, {}), {1}: (5, {})} | custom-call | flops 805306368 | bytes 1048576 | tf_op jit(solution)/shard_map/pallas_call | solution.py:193
  17.9 0.0 collective-permute-done.1.refs_4_.plus_ref
  17.9 0.7 collective-permute-done.4.refs_3_.minus_ref
  18.6 1.6 %collective-permute-start.7 = (f32[264,128]{1,0:T(8,128)S(1)}, f32[264,128]{1,0:T(8,128)S(1)}, u32[]{:S(2)}, u32[]{:S(2)}) collective-permute-start(f32[264,128]{1,0:T(8,128)S(1)} %shard_map.54), channel_id=1, source_target_pairs={{0,32},{1,97},{16,48},{17,113},{32,64},{33,1},{48,80},{49,17},{64,... | collective-permute-start | bytes 405512 | tf_op jit(solution)/shard_map/ppermute | solution.py:215
  20.2 0.7 collective-permute-start.2
  20.9 0.4 collective-permute-start.5
  21.3 0.0 collective-permute-done.6.refs_0_
  21.3 3.7 %shard_map.52 = (f32[8,2,256,1024]{3,2,1,0:T(8,128)S(1)}, bf16[2,768,1024]{2,1,0:T(8,128)(2,1)S(1)}, f32[2,2,8,1024]{3,2,1,0:T(8,128)S(1)}) custom-call(f32[1024,128]{1,0:T(8,128)S(1)} %collective-permute-done.6.refs_0_, bf16[3,256,768]{2,1,0:T(8,128)(2,1)S(1)} %get-tuple-element.24.refs_1_, ...), custom_call_target="tpu_custom_call", output_to_operand_aliasing={{0}: (5, {}), {1}: (6, {}), {2}: (7, {})} | custom-call | flops 2818572288 | bytes 1048576 | tf_op jit(solution)/shard_map/pallas_call | solution.py:193
  25.0 1.0 %collective-permute-done.2.refs_0_ = f32[264,128]{1,0:T(8,128)S(1)} collective-permute-done((f32[264,128]{1,0:T(8,128)S(1)}, f32[264,128]{1,0:T(8,128)S(1)}, u32[]{:S(2)}, u32[]{:S(2)}) %collective-permute-start.2) | collective-permute-done | bytes 135200 | tf_op jit(solution)/shard_map/ppermute | solution.py:336
  26.0 0.4 collective-permute-done.5.refs_1_
  26.4 2.2 %shard_map.53 = (f32[8,2,256,1024]{3,2,1,0:T(8,128)S(1)}, bf16[2,768,1024]{2,1,0:T(8,128)(2,1)S(1)}, f32[2,2,8,1024]{3,2,1,0:T(8,128)S(1)}) custom-call(f32[264,128]{1,0:T(8,128)S(1)} %collective-permute-done.2.refs_0_, f32[264,128]{1,0:T(8,128)S(1)} %collective-permute-done.5.refs_1_, ...), custom_call_target="tpu_custom_call", output_to_operand_aliasing={{0}: (2, {}), {1}: (3, {}), {2}: (4, {})} | custom-call | flops 1610612736 | bytes 1048576 | tf_op jit(solution)/shard_map/pallas_call | solution.py:193
  28.6 0.0 collective-permute-done.7.block_ref
  28.6 1.2 %shard_map.55 = (f32[8,2,256,1024]{3,2,1,0:T(8,128)S(1)}, f32[2,2,8,1024]{3,2,1,0:T(8,128)S(1)}, f32[32,2,8,128]{3,2,1,0:T(8,128)S(1)}) custom-call(bf16[2,768,1024]{2,1,0:T(8,128)(2,1)S(1)} %get-tuple-element.31.x_ref, f32[264,128]{1,0:T(8,128)S(1)} %collective-permute-done.7.block_ref, ...), custom_call_target="tpu_custom_call", output_to_operand_aliasing={{0}: (2, {}), {1}: (3, {})} | custom-call | flops 805306368 | bytes 1048576 | tf_op jit(solution)/shard_map/pallas_call | solution.py:193
  29.9 18.9 %all_to_all.20.rows_ref = f32[32,2,8,128]{3,2,1,0:T(8,128)S(1)} all-to-all(f32[32,2,8,128]{3,2,1,0:T(8,128)S(1)} %get-tuple-element.34), channel_id=1, replica_groups=mesh['xl'=2,'z'=8,'y'=4,'xh'=2,'core'=2] {'xl','y','xh','core'}, dimensions={0} | all-to-all | bytes 524288 | tf_op jit(solution)/shard_map/all_to_all | solution.py:340
  48.8 3.3 %shard_map.56 = f32[8,16,128]{2,1,0:T(8,128)S(1)} custom-call(f32[32,2,8,128]{3,2,1,0:T(8,128)S(1)} %all_to_all.20.rows_ref, f32[8,128]{1,0:T(8,128)S(1)} %get-tuple-element.35.src_norm_ref, f32[8,2,256,1024]{3,2,1,0:T(8,128)S(1)} %get-tuple-element.36.tile_ref), custom_call_target="tpu_custom_call" | custom-call | flops 6442450944 | bytes 1048576 | tf_op jit(solution)/shard_map/pallas_call | solution.py:193
  52.1 11.8 %all_to_all.21.cols_ref = f32[8,16,128]{2,1,0:T(8,128)S(1)} all-to-all(f32[8,16,128]{2,1,0:T(8,128)S(1)} %shard_map.56), channel_id=1, replica_groups=mesh['xl'=2,'z'=8,'y'=4,'xh'=2,'core'=2] {'z'}, dimensions={0} | all-to-all | bytes 131072 | tf_op jit(solution)/shard_map/all_to_all | solution.py:379
  64.0 3.8 %shard_map.57 = f32[32,2,8,128]{3,2,1,0:T(8,128)S(1)} custom-call(f32[8,16,128]{2,1,0:T(8,128)S(1)} %all_to_all.21.cols_ref, f32[8,2,256,1024]{3,2,1,0:T(8,128)S(1)} %get-tuple-element.36.tile_ref), custom_call_target="tpu_custom_call" | custom-call | flops 6442450944 | bytes 1048576 | tf_op jit(solution)/shard_map/pallas_call | solution.py:193
  67.8 13.8 %all_to_all.22.rows_ref = f32[32,2,8,128]{3,2,1,0:T(8,128)S(1)} all-to-all(f32[32,2,8,128]{3,2,1,0:T(8,128)S(1)} %shard_map.57), channel_id=1, replica_groups=mesh['xl'=2,'z'=8,'y'=4,'xh'=2,'core'=2] {'xl','y','xh','core'}, dimensions={0} | all-to-all | bytes 524288 | tf_op jit(solution)/shard_map/all_to_all | solution.py:340
  81.6 3.5 %shard_map.58 = (f32[8,2,128]{2,1,0:T(2,128)S(1)}, f32[8,128]{1,0:T(8,128)}) custom-call(f32[32,2,8,128]{3,2,1,0:T(8,128)S(1)} %all_to_all.22.rows_ref, f32[8,128]{1,0:T(8,128)S(1)} %get-tuple-element.35.src_norm_ref, f32[8,2,256,1024]{3,2,1,0:T(8,128)S(1)} %get-tuple-element.36.tile_ref), custom_call_target="tpu_custom_call" | custom-call | flops 6442450944 | bytes 1048576 | tf_op jit(solution)/shard_map/pallas_call | solution.py:193
  85.1 8.9 %all_to_all.23 = f32[8,2,128]{2,1,0:T(2,128)S(1)} all-to-all(f32[8,2,128]{2,1,0:T(2,128)S(1)} %get-tuple-element.38), channel_id=1, replica_groups=mesh['xl'=2,'z'=8,'y'=4,'xh'=2,'core'=2] {'z'}, dimensions={0} | all-to-all | bytes 16384 | tf_op jit(solution)/shard_map/all_to_all | solution.py:381
  94.1 0.6 add_bitcast_fusion
  (3 shorter events, 0.1 us)
Async XLA Ops:
  0.6 20.7 %collective-permute-start.6 = (f32[1024,128]{1,0:T(8,128)}, f32[1024,128]{1,0:T(8,128)S(1)}, u32[]{:S(2)}, u32[]{:S(2)}) collective-permute-start(f32[1024,128]{1,0:T(8,128)} %sources_ref.1), channel_id=1, source_target_pairs={{0,128},{128,0},{1,129},{129,1},{2,130},{130,2},{3,131},{131,3},{4... | collective-permute-start | bytes 1572872 | tf_op jit(solution)/shard_map/ppermute | solution.py:331
  3.7 8.7 %collective-permute-start = (f32[264,128]{1,0:T(8,128)S(1)}, f32[264,128]{1,0:T(8,128)S(1)}, u32[]{:S(2)}, u32[]{:S(2)}) collective-permute-start(f32[264,128]{1,0:T(8,128)S(1)} %select_maximum_fusion.block_ref.packed_ref), channel_id=1, source_target_pairs={{0,112},{16,32},{32,16},{48,64},{64,48},{80,96},{96,80},{112,0},{1... | collective-permute-start | bytes 405512 | tf_op jit(solution)/shard_map/ppermute | solution.py:336
  9.3 4.2 %collective-permute-start.3 = (f32[264,128]{1,0:T(8,128)S(1)}, f32[264,128]{1,0:T(8,128)S(1)}, u32[]{:S(2)}, u32[]{:S(2)}) collective-permute-start(f32[264,128]{1,0:T(8,128)S(1)} %select_maximum_fusion.block_ref.packed_ref), channel_id=1, source_target_pairs={{0,16},{16,0},{32,48},{48,32},{64,80},{80,64},{96,112},{112,96},{1... | collective-permute-start | bytes 405512 | tf_op jit(solution)/shard_map/ppermute | solution.py:336
  12.4 5.5 %collective-permute-start.1 = (f32[264,128]{1,0:T(8,128)S(1)}, f32[264,128]{1,0:T(8,128)S(1)}, u32[]{:S(2)}, u32[]{:S(2)}) collective-permute-start(f32[264,128]{1,0:T(8,128)S(1)} %collective-permute-done.minus_ref), channel_id=1, source_target_pairs={{0,16},{16,0},{32,48},{48,32},{64,80},{80,64},{96,112},{112,96},{1... | collective-permute-start | bytes 405512 | tf_op jit(solution)/shard_map/ppermute | solution.py:336
  13.5 5.1 %collective-permute-start.4 = (f32[264,128]{1,0:T(8,128)S(1)}, f32[264,128]{1,0:T(8,128)S(1)}, u32[]{:S(2)}, u32[]{:S(2)}) collective-permute-start(f32[264,128]{1,0:T(8,128)S(1)} %collective-permute-done.3.plus_ref), channel_id=1, source_target_pairs={{0,112},{16,32},{32,16},{48,64},{64,48},{80,96},{96,80},{112,0},{1... | collective-permute-start | bytes 405512 | tf_op jit(solution)/shard_map/ppermute | solution.py:336
  14.8 1.0 %copy-start = (f32[1024,128]{1,0:T(8,128)S(1)}, f32[1024,128]{1,0:T(8,128)}, u32[]{:S(2)}) copy-start(f32[1024,128]{1,0:T(8,128)} %sources_ref.1) | copy-start | bytes 1572868
  18.6 10.0 %collective-permute-start.7 = (f32[264,128]{1,0:T(8,128)S(1)}, f32[264,128]{1,0:T(8,128)S(1)}, u32[]{:S(2)}, u32[]{:S(2)}) collective-permute-start(f32[264,128]{1,0:T(8,128)S(1)} %shard_map.54), channel_id=1, source_target_pairs={{0,32},{1,97},{16,48},{17,113},{32,64},{33,1},{48,80},{49,17},{64,... | collective-permute-start | bytes 405512 | tf_op jit(solution)/shard_map/ppermute | solution.py:215
  20.2 5.8 %collective-permute-start.2 = (f32[264,128]{1,0:T(8,128)S(1)}, f32[264,128]{1,0:T(8,128)S(1)}, u32[]{:S(2)}, u32[]{:S(2)}) collective-permute-start(f32[264,128]{1,0:T(8,128)S(1)} %collective-permute-done.1.refs_4_.plus_ref), channel_id=1, source_target_pairs={{0,112},{16,32},{32,16},{48,64},{64,48},{80,96},{96,80},{112,0},{1... | collective-permute-start | bytes 405512 | tf_op jit(solution)/shard_map/ppermute | solution.py:336
  20.9 5.5 %collective-permute-start.5 = (f32[264,128]{1,0:T(8,128)S(1)}, f32[264,128]{1,0:T(8,128)S(1)}, u32[]{:S(2)}, u32[]{:S(2)}) collective-permute-start(f32[264,128]{1,0:T(8,128)S(1)} %collective-permute-done.4.refs_3_.minus_ref), channel_id=1, source_target_pairs={{0,16},{16,0},{32,48},{48,32},{64,80},{80,64},{96,112},{112,96},{1... | collective-permute-start | bytes 405512 | tf_op jit(solution)/shard_map/ppermute | solution.py:336
